TPU v7x, 8 devices: a whole 2x2x1 slice. The times are simulated.
8 devices in a mesh: data: 1 (over z), model: 2 (over y), seq: 4 (over x, core).
Axes of the slice: x: 2, y: 2, z: 1, core: 2. Of those that a mesh axis runs over, the one named last changes fastest.
Arguments:
- tokens: bfloat16 [64, 4096, 384], P('data', 'seq')
- lengths: int32 [64], P('data')
- slot_params: bfloat16 [384, 256], replicated
- logit_scale: float32 [], replicated
- w_in: bfloat16 [256, 384, 1536], P('seq', None, 'model')
- w_out: bfloat16 [256, 1536, 384], P('seq', 'model')
Outputs:
- output: bfloat16 [64, 4096, 384], P('data', 'seq')
All inputs are finite; a program needn't handle non-finite values.
Results may differ from a plain program's by a relative error of at most 0.0158228.
Values are sent between devices in bfloat16 or wider.
A program may use at most 1 GiB of HBM per device.

v0:
```python
import jax
import jax.numpy as jnp
from jax import lax
from jax.sharding import PartitionSpec as P

NORM_EPS = 1e-6


def unit_vectors(values, axis):
    v32 = values.astype(jnp.float32)
    return (v32 * lax.rsqrt(jnp.sum(v32 * v32, axis=axis, keepdims=True) + NORM_EPS)).astype(jnp.bfloat16)


def solution(mesh):
    seq_size = mesh.shape["seq"]

    def local_layer(tokens, lengths, slot_params, logit_scale, w_in, w_out):
        batch_size, tok_count, model_dim = tokens.shape
        n_slots = slot_params.shape[1]
        local_experts = w_in.shape[0]
        local_slots = n_slots // seq_size
        slot_per = local_slots // local_experts
        positions = lax.axis_index("seq") * tok_count + jnp.arange(tok_count)
        is_valid = positions[None, :] < lengths[:, None]
        logits = logit_scale * jnp.einsum("bmd,dn->bmn", unit_vectors(tokens, 2), unit_vectors(slot_params, 0), preferred_element_type=jnp.float32)
        masked = jnp.where(is_valid[:, :, None], logits, -1e30)
        col_max = lax.pmax(jnp.max(masked, axis=1, keepdims=True), "seq")
        weights = jnp.exp(masked - col_max)
        col_sum = lax.psum_scatter(jnp.sum(weights, axis=1), "seq", scatter_dimension=1, tiled=True)
        part_sum = jnp.einsum("bmn,bmd->bnd", weights.astype(jnp.bfloat16), tokens, preferred_element_type=jnp.float32)
        slot_sum = lax.psum_scatter(part_sum.astype(jnp.bfloat16), "seq", scatter_dimension=1, tiled=True)
        slot_in = (slot_sum.astype(jnp.float32) / col_sum[:, :, None]).astype(jnp.bfloat16)
        grouped = slot_in.reshape(batch_size, local_experts, slot_per, model_dim)
        hidden = jnp.einsum("besd,edf->besf", grouped, w_in, preferred_element_type=jnp.float32)
        hidden = jax.nn.gelu(hidden, approximate=False).astype(jnp.bfloat16)
        out_part = jnp.einsum("besf,efd->besd", hidden, w_out, preferred_element_type=jnp.float32)
        slot_out = lax.psum(out_part, "model").astype(jnp.bfloat16).reshape(batch_size, local_slots, model_dim)
        all_slots = lax.all_gather(slot_out, "seq", axis=1, tiled=True)
        mix_weights = jax.nn.softmax(logits, axis=-1).astype(jnp.bfloat16)
        mixed = jnp.einsum("bmn,bnd->bmd", mix_weights, all_slots, preferred_element_type=jnp.float32)
        return jnp.where(is_valid[:, :, None], mixed, 0.0).astype(jnp.bfloat16)

    return jax.shard_map(local_layer, mesh=mesh, in_specs=(P("data", "seq", None), P("data"), P(), P(), P("seq", None, "model"), P("seq", "model", None)), out_specs=P("data", "seq", None), check_vma=False)
```

profile of v0, /device:TPU:0, one launch (start us, length us, event | category | flops | bytes accessed | tf_op | source)
XLA Modules:
  0.0 610.8 jit_solution(11491158943203057989)
XLA Ops:
  6.5 0.0 all-reduce.3.cloned.1.call-start
  7.2 1.0 fusion.76
  8.2 0.0 copy-start.4
  8.2 0.0 copy-start.2
  8.2 29.9 %fusion.1 = f32[64,1024]{1,0:T(8,128)S(1)} fusion(bf16[64,1024,384]{2,1,0:T(8,128)(2,1)} %param.6), kind=kLoop, calls=%fused_computation.3 | loop fusion | flops 75431936 | bytes 50593792 | tf_op jit(solution)/shard_map/reduce_sum | solution.py:11
  38.2 0.0 copy-done.4
  38.2 0.1 broadcast_compare_fusion
  38.4 0.0 copy-done.2
  38.4 0.0 copy-start
  38.4 43.4 %select_reduce_fusion = (f32[64,256]{1,0:T(8,128)}, f32[64,1024,256]{2,1,0:T(8,128)}) fusion(f32[]{:T(128)S(6)} %copy.28, pred[64,1024]{1,0:T(8,128)(4,1)S(1)} %broadcast_compare_fusion, bf16[384,256]{1,0:T(8,128)(2,1)S(1)} %copy-done.2, f32[256]{0:T(256)S(1)} %add_rsqrt_fusion.1, bf16[64,1024,384]{2,1,0:T(8,128)(2,1)} %param.6, ...), kind=kOutput, calls=%fused_computation.9 | convolution fusion | flops 13011009536 | bytes 118031360 | tf_op jit(solution)/shard_map/bmd,dn->bmn/dot_general | solution.py:25
  81.8 0.0 all-reduce.3.cloned.1.call-update
  81.8 0.0 reduce-scatter.7.cloned.1.call-start
  81.8 28.9 %all-reduce.3.cloned.1.call-done = f32[64,256]{1,0:T(8,128)} async-done(((f32[64,256]{1,0:T(8,128)}), f32[64,256]{1,0:T(8,128)}) %all-reduce.3.cloned.1.call-update) | async-done | bytes 65552 | tf_op jit(solution)/shard_map/pmax | solution.py:27
  110.7 0.0 copy-start.3
  110.7 21.1 %fusion.3 = f32[64,256]{1,0:T(8,128)S(1)} fusion(f32[64,1024,256]{2,1,0:T(8,128)} %get-tuple-element.8, f32[64,256]{1,0:T(8,128)} %all-reduce.3.cloned.1.call-done, f32[]{:T(128)S(6)} %copy.28, pred[64,1024]{1,0:T(8,128)(4,1)S(1)} %broadcast_compare_fusion), kind=kLoop, calls=%fused_computation.10 | loop fusion | flops 67092480 | bytes 67305472 | tf_op jit(solution)/shard_map/reduce_sum | solution.py:29
  131.8 0.7 copy.16
  132.6 0.0 reduce-scatter.7.cloned.1.call-update
  132.6 0.0 reduce-scatter.5.cloned.1.call-start
  132.6 0.0 copy-done
  132.7 0.0 copy-done.3
  132.7 44.6 %fusion.36 = bf16[64,256,384]{2,1,0:T(8,128)(2,1)} fusion(bf16[64,1024,384]{2,1,0:T(8,128)(2,1)} %param.6, f32[64,1024,256]{2,1,0:T(8,128)} %get-tuple-element.8, f32[64,256]{1,0:T(8,128)S(1)} %copy-done.3, f32[]{:T(128)S(6)} %copy.28, pred[64,1024]{1,0:T(8,128)(4,1)S(1)} %broadcast_compare_fusion), kind=kOutput, calls=%fused_computation.46 | convolution fusion | flops 12958302208 | bytes 130154496 | tf_op jit(solution)/shard_map/bmn,bmd->bnd/dot_general | solution.py:30
  177.2 0.0 reduce-scatter.5.cloned.1.call-update
  177.3 0.2 all-gather.3.cloned.1.call-start
  177.5 0.0 reduce-scatter.7.cloned.1.call-done
  177.5 0.8 copy.17
  178.3 89.6 %reduce-scatter.5.cloned.1.call-done = bf16[64,64,384]{2,1,0:T(8,128)(2,1)} async-done(((bf16[64,256,384]{2,1,0:T(8,128)(2,1)}), bf16[64,64,384]{2,1,0:T(8,128)(2,1)}) %reduce-scatter.5.cloned.1.call-update) | async-done | bytes 3145744 | tf_op jit(solution)/shard_map/reduce_scatter | solution.py:31
  268.0 2.4 divide_convert_fusion.4
  270.3 19.2 %fusion.71 = f32[64,64,768]{2,1,0:T(8,128)} fusion(bf16[64,384,768]{2,1,0:T(8,128)(2,1)} %param.10, bf16[64,64,384]{2,1,0:T(8,128)(2,1)S(1)} %divide_convert_fusion.4), kind=kOutput, calls=%fused_computation.79 | convolution fusion | flops 2415919104 | bytes 53477376 | tf_op jit(solution)/shard_map/besd,edf->besf/dot_general | solution.py:34
  289.5 33.6 %fusion.73 = f32[64,64,1,384]{3,0,1,2:T(8,128)} fusion(bf16[64,768,384]{2,1,0:T(8,128)(2,1)} %param.11, f32[64,64,768]{2,1,0:T(8,128)} %fusion.71), kind=kOutput, calls=%fused_computation.82 | convolution fusion | flops 2620391424 | bytes 56623104 | tf_op jit(solution)/shard_map/besf,efd->besd/dot_general | solution.py:36
  323.0 147.7 %all-reduce.4 = bf16[64,64,1,384]{3,0,1,2:T(8,128)(2,1)} all-reduce(f32[64,64,1,384]{3,0,1,2:T(8,128)} %fusion.73), channel_id=1, replica_groups=mesh['data'=1,'model'=2,'seq'=4] {'model'}, use_global_device_ids=true, to_apply=%region_9.10 | all-reduce | flops 1572864 | bytes 9437184 | tf_op jit(solution)/shard_map/psum | solution.py:37
  470.7 0.0 all-gather.3.cloned.1.call-update
  470.7 0.0 copy-start.1
  470.8 69.0 %fusion.112 = (f32[64,1024]{1,0:T(8,128)S(1)}, f32[64,1024,256]{2,1,0:T(8,128)}) fusion(f32[64,1024,256]{2,1,0:T(8,128)} %get-tuple-element.8, f32[]{:T(128)S(6)} %copy.28), kind=kOutput, calls=%fused_computation.124 | output fusion | flops 67109120 | bytes 134479872 | tf_op jit(solution)/shard_map/sub | solution.py:39
  539.8 10.5 %all-gather.3.cloned.1.call-done = bf16[64,256,1,384]{3,0,2,1:T(8,128)(2,1)} async-done(((bf16[64,64,1,384]{3,0,2,1:T(8,128)(2,1)}), bf16[64,256,1,384]{3,0,2,1:T(8,128)(2,1)}) %all-gather.3.cloned.1.call-update) | async-done | bytes 12582928 | tf_op jit(solution)/shard_map/all_gather | solution.py:38
  550.2 0.0 copy-done.1
  550.2 54.0 %select_convert_fusion = bf16[64,1024,384]{2,1,0:T(8,128)(2,1)} fusion(pred[64,1024]{1,0:T(8,128)(4,1)S(1)} %copy-done.1, f32[64,1024,256]{2,1,0:T(8,128)} %get-tuple-element.6, f32[64,1024]{1,0:T(8,128)S(1)} %get-tuple-element.5, bf16[64,256,1,384]{3,0,2,1:T(8,128)(2,1)} %all-gather.3.cloned.1.call-done), kind=kOutput, calls=%fused_computation.5 | convolution fusion | flops 12968787968 | bytes 130351104 | tf_op jit(solution)/shard_map/bmn,bnd->bmd/dot_general | solution.py:40
  (3 shorter events, 0.1 us)
Async XLA Ops:
  6.5 104.2 %all-reduce.3.cloned.1.call-start = ((), (), s32[]{:S(2)}) async-start(), calls=%async_computation.2 | async-start | bytes 131072 | tf_op jit(solution)/shard_map/pmax | solution.py:27
  8.2 30.0 %copy-start.4 = (s32[64]{0:T(128)S(1)}, s32[64]{0:T(128)}, u32[]{:S(2)}) copy-start(s32[64]{0:T(128)} %param.7) | copy-start | bytes 772
  8.2 30.1 %copy-start.2 = (bf16[384,256]{1,0:T(8,128)(2,1)S(1)}, bf16[384,256]{1,0:T(8,128)(2,1)}, u32[]{:S(2)}) copy-start(bf16[384,256]{1,0:T(8,128)(2,1)} %param.8) | copy-start | bytes 589828
  38.4 94.3 %copy-start = (pred[64,1024]{1,0:T(8,128)(4,1)}, pred[64,1024]{1,0:T(8,128)(4,1)S(1)}, u32[]{:S(2)}) copy-start(pred[64,1024]{1,0:T(8,128)(4,1)S(1)} %broadcast_compare_fusion) | copy-start | bytes 196612
  81.8 95.7 %reduce-scatter.7.cloned.1.call-start = ((), (), s32[]{:S(2)}) async-start(), calls=%async_computation.5 | async-start | bytes 163840
  110.7 22.0 %copy-start.3 = (f32[64,256]{1,0:T(8,128)S(1)}, f32[64,256]{1,0:T(8,128)}, u32[]{:S(2)}) copy-start(f32[64,256]{1,0:T(8,128)} %all-reduce.3.cloned.1.call-done) | copy-start | bytes 196612
  132.6 135.4 %reduce-scatter.5.cloned.1.call-start = ((), (), s32[]{:S(2)}) async-start(), calls=%async_computation.3 | async-start | bytes 15728640 | tf_op jit(solution)/shard_map/reduce_scatter | solution.py:31
  177.3 373.0 %all-gather.3.cloned.1.call-start = ((), (), s32[]{:S(2)}) async-start(), calls=%async_computation.4 | async-start | bytes 15728640 | tf_op jit(solution)/shard_map/all_gather | solution.py:38
  470.7 79.5 %copy-start.1 = (pred[64,1024]{1,0:T(8,128)(4,1)S(1)}, pred[64,1024]{1,0:T(8,128)(4,1)}, u32[]{:S(2)}) copy-start(pred[64,1024]{1,0:T(8,128)(4,1)} %copy-done) | copy-start | bytes 196612
Sparse Core Ops, SparseCore 0:
  81.9 28.7 all-reduce.2
  132.7 14.0 reduce-scatter.6
  177.4 90.5 reduce-scatter.4
  470.9 79.3 all-gather.2
where the time goes:
time: 611 us
  matrix products  195 us (32%)
  blocking collectives  148 us (24%)
  waiting for transfers between devices  129 us (21%)
  other arithmetic  124 us (20%)
  between operations  13.9 us (2%)
    psum x1, blocking collectives, local_layer(): lax.psum(out_part, 'model').astype(jnp.bfloat16)  148 us
    reduce_scatter x1, waiting for transfers between devices, local_layer(): lax.psum_scatter(part_sum.astype(jnp.bfloat16), 'seq', scatter_dimension=...  89.6 us
    sub x1, other arithmetic, local_layer(): mix_weights = jax.nn.softmax(logits, axis=-1).astype(jnp.bfloat16)  69 us
    dot_general x1, matrix products, local_layer(): jnp.einsum('bmn,bnd->bmd', mix_weights, all_slots, preferred_element_type...  54 us
    dot_general x1, matrix products, local_layer(): jnp.einsum('bmn,bmd->bnd', weights.astype(jnp.bfloat16), tokens, preferre...  44.6 us
    dot_general x1, matrix products, local_layer(): jnp.einsum('bmd,dn->bmn', unit_vectors(tokens, 2), unit_vectors(slot_para...  43.4 us
    dot_general x1, matrix products, local_layer(): jnp.einsum('besf,efd->besd', hidden, w_out, preferred_element_type=jnp.fl...  33.6 us
    reduce_sum x2, other arithmetic, unit_vectors(): jnp.sum(v32 * v32, axis=axis, keepdims=True) + NORM_EPS  30.9 us
  transfers between devices with their start and end apart: 4, of which 3 were waited for; matrix products, arithmetic and copies ran while one was open for 19% of the time, Pallas kernels for 0%

commit v1 on v0

v1 whole, which is shorter than its diff:
```python
import functools
import math
import jax
import jax.numpy as jnp
from jax import lax
from jax.experimental import pallas as pl
from jax.experimental.pallas import tpu as pltpu
from jax.sharding import PartitionSpec as P

NORM_EPS = 1e-6
LOG2E = math.log2(math.e)
MASKED = -1e30
MESH = pl.DeviceIdType.MESH
F32, BF16 = jnp.float32, jnp.bfloat16
NT = (((1,), (1,)), ((), ()))


def unit_vectors(values, axis):
    v32 = values.astype(F32)
    return (v32 * lax.rsqrt(jnp.sum(v32 * v32, axis=axis, keepdims=True) + NORM_EPS)).astype(BF16)


def place():
    y, s = lax.axis_index("model"), lax.axis_index("seq")
    x, core = s // 2, lax.rem(s, 2)
    partner = (0, y, x * 2 + 1 - core)
    across_x = (0, y, (1 - x) * 2 + core)
    across_y = (0, 1 - y, s)
    return y, x, core, s, partner, across_x, across_y


def greet(devices):
    barrier = pltpu.get_barrier_semaphore()
    for device in devices:
        pl.semaphore_signal(barrier, inc=1, device_id=device, device_id_type=MESH)
    pl.semaphore_wait(barrier, len(devices))


def remote(src, dst, send, recv, device):
    return pltpu.make_async_remote_copy(src_ref=src, dst_ref=dst, send_sem=send, recv_sem=recv, device_id=device, device_id_type=MESH)


def merge_weights(a, b):
    top = jnp.maximum(a, b)
    ea, eb = jnp.exp2(a - top), jnp.exp2(b - top)
    total = ea + eb
    row = lax.broadcasted_iota(jnp.int32, (8, a.shape[1]), 0)
    weights = jnp.where(row == 0, ea / total, eb / total)
    return jnp.transpose(weights), top + jnp.log2(total)


def scatter_rows(acc, first, stride, rows):
    for j in range(acc.shape[0]):
        acc[j, pl.ds(first, rows.shape[0], stride=stride), :] = rows[:, j * 128 : (j + 1) * 128]


def gather_rows(acc, rows):
    return jnp.concatenate([acc[j, rows, :] for j in range(acc.shape[0])], axis=1)


def dispatch_kernel(half, x_hbm, vt_ref, len_ref, kg_ref, xs_ref, xbuf, part, dpart, mid, xpart, own, yown, acc, lse, dlse, mlse, xlse, wcol, in_sem, d_s, d_r, dl_s, dl_r, x_s, x_r, xl_s, xl_r, y_s, y_r):
    tok, n_slots, dim = xbuf.shape[1], vt_ref.shape[0], xbuf.shape[2]
    core_slots, dev_slots = n_slots // 2, n_slots // 4
    n_batch = 2 * half
    y, x, core, s, partner, across_x, across_y = place()
    base = y * half
    ring = xbuf.shape[0]

    def load(i):
        slot = lax.rem(i, ring)
        return pltpu.make_async_copy(x_hbm.at[base + i], xbuf.at[slot], in_sem.at[slot])

    def core_copy(i):
        rows = pl.ds(pl.multiple_of((1 - core) * core_slots, core_slots), core_slots)
        return remote(part.at[i, rows], dpart.at[i], d_s.at[i], d_r.at[i], partner)

    def core_lse(i):
        return remote(lse.at[i, 1 - core], dlse.at[i], dl_s.at[i], dl_r.at[i], partner)

    def x_copy(i):
        rows = pl.ds(pl.multiple_of((1 - x) * dev_slots, dev_slots), dev_slots)
        return remote(mid.at[i, rows], xpart.at[i], x_s.at[i], x_r.at[i], across_x)

    def x_lse(i):
        return remote(mlse.at[i], xlse.at[i], xl_s.at[i], xl_r.at[i], across_x)

    def y_copy(i):
        return remote(own.at[i], yown.at[i], y_s.at[i], y_r.at[i], across_y)

    for i in range(ring):
        load(i).start()
    greet((partner, across_x, across_y))

    def step(i, carry):
        @pl.when(i < half)
        def _():
            load(i).wait()
            slot = lax.rem(i, ring)
            xv = xbuf[slot]
            xf = xv.astype(F32)
            square = jnp.sum(xf * xf, axis=1, keepdims=True)
            square_row = jnp.transpose(jnp.broadcast_to(square, (tok, 128)))[0:1]
            scale_row = lax.rsqrt(square_row + NORM_EPS) * kg_ref[0]
            logits = lax.dot_general(vt_ref[...], xv, NT, preferred_element_type=F32) * scale_row
            lane = lax.broadcasted_iota(jnp.int32, (1, tok), 1)
            masked = jnp.where(lane < len_ref[base + i] - s * tok, logits, MASKED)
            top = jnp.max(masked, axis=1, keepdims=True)
            weights = jnp.exp2(masked - top)
            total = jnp.sum(weights, axis=1, keepdims=True)
            mean = jnp.dot(weights.astype(BF16), xv, preferred_element_type=F32) * (1.0 / total)
            part[i] = mean.astype(BF16)
            first = lax.broadcasted_iota(jnp.int32, (n_slots, 128), 1) == 0
            rows = jnp.transpose(jnp.where(first, top, total))
            row = rows[0:1] + jnp.log2(rows[1:2])
            lse[i, 0] = row[:, :128]
            lse[i, 1] = row[:, 128:]
            core_copy(i).start()
            core_lse(i).start()

            @pl.when(i + ring < half)
            def _():
                load(i + ring).start()

        @pl.when((i >= 1) & (i < half + 1))
        def _():
            k = i - 1
            core_copy(k).wait_recv()
            core_lse(k).wait_recv()
            cols, row = merge_weights(lse[k, core], dlse[k])
            rows = pl.ds(pl.multiple_of(core * core_slots, core_slots), core_slots)
            merged = cols[:, 0:1] * part[k, rows].astype(F32) + cols[:, 1:2] * dpart[k].astype(F32)
            mid[k] = merged.astype(BF16)
            mlse[k] = row
            x_copy(k).start()
            x_lse(k).start()

        @pl.when((i >= 4) & (i < half + 4))
        def _():
            k = i - 4
            x_copy(k).wait_recv()
            x_lse(k).wait_recv()
            cols, _ = merge_weights(mlse[k], xlse[k])
            wcol[...] = cols
            rows = pl.ds(pl.multiple_of(x * dev_slots, dev_slots), dev_slots)
            mine = wcol[rows, :]
            merged = mine[:, 0:1] * mid[k, rows].astype(F32) + mine[:, 1:2] * xpart[k].astype(F32)
            own[k] = merged.astype(BF16)
            y_copy(k).start()
            scatter_rows(acc, base + k, n_batch, merged)

        @pl.when(i >= 7)
        def _():
            k = i - 7
            y_copy(k).wait_recv()
            scatter_rows(acc, (1 - y) * half + k, n_batch, yown[k].astype(F32))

        return carry

    lax.fori_loop(0, half + 7, step, 0)

    def flush(e, carry):
        rows = pl.ds(pl.multiple_of(e * n_batch, n_batch), n_batch)
        xs_ref[rows, :] = gather_rows(acc, rows).astype(BF16)
        return carry

    lax.fori_loop(0, dev_slots, flush, 0)

    def drain(i, carry):
        core_copy(i).wait_send()
        core_lse(i).wait_send()
        x_copy(i).wait_send()
        x_lse(i).wait_send()
        y_copy(i).wait_send()
        return carry

    lax.fori_loop(0, half, drain, 0)


def dispatch(tokens, vt, lengths, kg):
    n_batch, tok, dim = tokens.shape
    n_slots = vt.shape[0]
    half, ring = n_batch // 2, 4
    dma = pltpu.SemaphoreType.DMA
    return pl.pallas_call(
        functools.partial(dispatch_kernel, half),
        out_shape=pltpu.VMEM((n_slots // 4 * n_batch, dim), BF16),
        in_specs=[pl.BlockSpec(memory_space=pl.ANY), pl.BlockSpec(memory_space=pltpu.VMEM), pl.BlockSpec(memory_space=pltpu.SMEM), pl.BlockSpec(memory_space=pltpu.SMEM)],
        out_specs=pl.BlockSpec(memory_space=pltpu.VMEM),
        scratch_shapes=[
            pltpu.VMEM((ring, tok, dim), BF16),
            pltpu.VMEM((half, n_slots, dim), BF16),
            pltpu.VMEM((half, n_slots // 2, dim), BF16),
            pltpu.VMEM((half, n_slots // 2, dim), BF16),
            pltpu.VMEM((half, n_slots // 4, dim), BF16),
            pltpu.VMEM((half, n_slots // 4, dim), BF16),
            pltpu.VMEM((half, n_slots // 4, dim), BF16),
            pltpu.VMEM((dim // 128, n_slots // 4 * n_batch, 128), F32),
            pltpu.VMEM((half, 2, 1, n_slots // 2), F32),
            pltpu.VMEM((half, 1, n_slots // 2), F32),
            pltpu.VMEM((half, 1, n_slots // 2), F32),
            pltpu.VMEM((half, 1, n_slots // 2), F32),
            pltpu.VMEM((n_slots // 2, 8), F32),
            dma((ring,)),
        ] + [dma((half,))] * 10,
        compiler_params=pltpu.CompilerParams(collective_id=0, has_side_effects=True, vmem_limit_bytes=48 << 20),
        name="dispatch",
    )(tokens, vt, lengths, kg)


def expert_kernel(n_group, n_chunk, x_hbm, v_ref, len_ref, kg_ref, xs_ref, win_hbm, wout_hbm, c_ref, ys_hbm, xbuf, wi, wo, acc, ysend, yrecv, x_sem, wi_sem, wo_sem, y_s, y_r, x_s, x_r, d_s, d_r, r_s, r_r, l_s):
    n_batch, tok, dim = x_hbm.shape
    n_expert = win_hbm.shape[0]
    group = n_expert // n_group
    sub = n_batch // n_chunk
    core_slots, dev_slots = 2 * n_expert, n_expert
    y, x, core, s, partner, across_x, across_y = place()
    x_ring, w_ring = xbuf.shape[0], wi.shape[0]
    n_pair = n_expert // 2
    n_q = n_group * n_chunk

    def load_x(b):
        slot = lax.rem(b, x_ring)
        return pltpu.make_async_copy(x_hbm.at[b], xbuf.at[slot], x_sem.at[slot])

    def load_w(p):
        slot = lax.rem(p, w_ring)
        return (
            pltpu.make_async_copy(win_hbm.at[pl.ds(2 * p, 2)], wi.at[slot], wi_sem.at[slot]),
            pltpu.make_async_copy(wout_hbm.at[pl.ds(2 * p, 2)], wo.at[slot], wo_sem.at[slot]),
        )

    def home(q, on_core, on_x):
        g, bq = q // n_chunk, lax.rem(q, n_chunk)
        slot0 = pl.multiple_of(on_core * core_slots + on_x * dev_slots + g * group, group)
        return ys_hbm.at[pl.ds(bq * sub, sub), pl.ds(slot0, group)]

    def y_copy(q):
        return remote(ysend.at[q], yrecv.at[q], y_s.at[q], y_r.at[q], across_y)

    def x_copy(q):
        return remote(yrecv.at[q], home(q, core, x), x_s.at[q], x_r.at[q], across_x)

    def x_arrival(q):
        return remote(yrecv.at[q], home(q, core, 1 - x), x_s.at[q], x_r.at[q], across_x)

    def core_copy(q):
        return remote(yrecv.at[q], home(q, core, x), d_s.at[q], d_r.at[q], partner)

    def core_arrival(q):
        return remote(yrecv.at[q], home(q, 1 - core, x), d_s.at[q], d_r.at[q], partner)

    def relay(q):
        return remote(home(q, core, 1 - x), home(q, core, 1 - x), r_s.at[q], r_r.at[q], partner)

    def relay_arrival(q):
        return remote(home(q, 1 - core, 1 - x), home(q, 1 - core, 1 - x), r_s.at[q], r_r.at[q], partner)

    def local_copy(q):
        return pltpu.make_async_copy(yrecv.at[q], home(q, core, x), l_s.at[q])

    for p in range(w_ring):
        for copy in load_w(p):
            copy.start()
    for b in range(x_ring):
        load_x(b).start()
    greet((partner, across_x, across_y))

    def expert_pair(p, carry):
        for copy in load_w(p):
            copy.wait()
        slot = lax.rem(p, w_ring)
        for j in range(2):
            e = 2 * p + j
            rows = xs_ref[pl.ds(pl.multiple_of(e * n_batch, n_batch), n_batch), :]
            hidden = jnp.dot(rows, wi[slot, j], preferred_element_type=F32)
            hidden = (0.5 * hidden * (1.0 + lax.erf(hidden * math.sqrt(0.5)))).astype(BF16)
            out = jnp.dot(hidden, wo[slot, j], preferred_element_type=F32)
            scatter_rows(acc, lax.rem(e, group), group, out)

        @pl.when(p + w_ring < n_pair)
        def _():
            for copy in load_w(p + w_ring):
                copy.start()

        return carry

    def mix_block(b, carry):
        load_x(b).wait()
        slot = lax.rem(b, x_ring)
        xv = xbuf[slot]
        xf = xv.astype(F32)
        scale = lax.rsqrt(jnp.sum(xf * xf, axis=1, keepdims=True) + NORM_EPS) * kg_ref[0]
        logits = jnp.dot(xv, v_ref[...], preferred_element_type=F32) * scale
        weights = jnp.exp2(logits - jnp.max(logits, axis=1, keepdims=True))
        valid = lax.broadcasted_iota(jnp.int32, (tok, 1), 0) < len_ref[b] - s * tok
        inverse = jnp.where(valid, 1.0 / jnp.sum(weights, axis=1, keepdims=True), 0.0)
        c_ref[b] = (weights * inverse).astype(BF16)

        @pl.when(b + x_ring < n_batch)
        def _():
            load_x(b + x_ring).start()

        return carry

    per = n_expert // n_q

    def step(t, carry):
        @pl.when(t < n_q)
        def _():
            lax.fori_loop(t * (per // 2), (t + 1) * (per // 2), expert_pair, 0)

        @pl.when((t < n_q) & (lax.rem(t, n_chunk) == n_chunk - 1))
        def _():
            g = t // n_chunk

            def pack(bq, carry):
                rows = gather_rows(acc, pl.ds(pl.multiple_of(bq * sub * group, sub * group), sub * group))
                q = g * n_chunk + bq
                ysend[q] = rows.reshape(sub, group, dim).astype(BF16)
                y_copy(q).start()
                return carry

            lax.fori_loop(0, n_chunk, pack, 0)

        @pl.when((t >= n_chunk) & (t < n_q + n_chunk))
        def _():
            k = (t - n_chunk) * (n_batch // n_q)
            lax.fori_loop(k, k + n_batch // n_q, mix_block, 0)

        @pl.when((t >= n_chunk) & (t < n_q + n_chunk))
        def _():
            q = t - n_chunk
            y_copy(q).wait_recv()
            yrecv[q] = (ysend[q].astype(F32) + yrecv[q].astype(F32)).astype(BF16)
            x_copy(q).start()
            core_copy(q).start()
            local_copy(q).start()

        @pl.when(t >= n_chunk + 1)
        def _():
            q = t - n_chunk - 1
            x_arrival(q).wait_recv()
            relay(q).start()

        return carry

    lax.fori_loop(0, n_q + n_chunk + 1, step, 0)

    def drain(q, carry):
        core_arrival(q).wait_recv()
        relay_arrival(q).wait_recv()
        y_copy(q).wait_send()
        x_copy(q).wait_send()
        core_copy(q).wait_send()
        relay(q).wait_send()
        local_copy(q).wait()
        return carry

    lax.fori_loop(0, n_q, drain, 0)


def experts(tokens, v, lengths, kg, xs, w_in, w_out):
    n_batch, tok, dim = tokens.shape
    n_slots = v.shape[1]
    n_expert, _, hid = w_in.shape
    n_group, n_chunk = 4, 4
    group, sub = n_expert // n_group, n_batch // n_chunk
    n_q = n_group * n_chunk
    x_ring, w_ring = 3, 3
    dma = pltpu.SemaphoreType.DMA
    vmem, smem, anym = pl.BlockSpec(memory_space=pltpu.VMEM), pl.BlockSpec(memory_space=pltpu.SMEM), pl.BlockSpec(memory_space=pl.ANY)
    return pl.pallas_call(
        functools.partial(expert_kernel, n_group, n_chunk),
        out_shape=(pltpu.VMEM((n_batch, tok, n_slots), BF16), jax.ShapeDtypeStruct((n_batch, n_slots, dim), BF16)),
        in_specs=[anym, vmem, smem, smem, vmem, anym, anym],
        out_specs=(vmem, anym),
        scratch_shapes=[
            pltpu.VMEM((x_ring, tok, dim), BF16),
            pltpu.VMEM((w_ring, 2, dim, hid), BF16),
            pltpu.VMEM((w_ring, 2, hid, dim), BF16),
            pltpu.VMEM((dim // 128, group * n_batch, 128), F32),
            pltpu.VMEM((n_q, sub, group, dim), BF16),
            pltpu.VMEM((n_q, sub, group, dim), BF16),
            dma((x_ring,)),
            dma((w_ring,)),
            dma((w_ring,)),
        ] + [dma((n_q,))] * 9,
        compiler_params=pltpu.CompilerParams(collective_id=1, has_side_effects=True, vmem_limit_bytes=24 << 20),
        name="experts",
    )(tokens, v, lengths, kg, xs, w_in, w_out)


def combine_kernel(step, c_ref, ys_ref, y_ref):
    first = pl.program_id(0) * step
    for j in range(step):
        y_ref[j] = jnp.dot(c_ref[first + j], ys_ref[j], preferred_element_type=F32).astype(BF16)


def combine(c, ys):
    n_batch, tok, n_slots = c.shape
    dim = ys.shape[2]
    step = 4
    return pl.pallas_call(
        functools.partial(combine_kernel, step),
        grid=(n_batch // step,),
        out_shape=jax.ShapeDtypeStruct((n_batch, tok, dim), BF16),
        in_specs=[pl.BlockSpec(memory_space=pltpu.VMEM), pl.BlockSpec((step, n_slots, dim), lambda i: (i, 0, 0))],
        out_specs=pl.BlockSpec((step, tok, dim), lambda i: (i, 0, 0)),
        compiler_params=pltpu.CompilerParams(vmem_limit_bytes=24 << 20),
        name="combine",
    )(c, ys)


def solution(mesh):
    def local_layer(tokens, lengths, slot_params, logit_scale, w_in, w_out):
        dim, n_slots = slot_params.shape
        v = unit_vectors(slot_params, 0)
        v = v.reshape(dim, 2, 2, n_slots // 4).transpose(0, 2, 1, 3).reshape(dim, n_slots)
        kg = (logit_scale * LOG2E).reshape(1)
        xs = pltpu.with_memory_space_constraint(dispatch(tokens, v.T, lengths, kg), pltpu.VMEM)
        c, ys = experts(tokens, v, lengths, kg, xs, w_in, w_out)
        return combine(pltpu.with_memory_space_constraint(c, pltpu.VMEM), ys)

    return jax.shard_map(local_layer, mesh=mesh, in_specs=(P("data", "seq", None), P("data"), P(), P(), P("seq", None, "model"), P("seq", "model", None)), out_specs=P("data", "seq", None), check_vma=False)
```

time: 611 us -> 193 us (0.32)
  matrix products: 195 us -> 0 us
  Pallas kernels: 0 us -> 189 us
  blocking collectives: 148 us -> 0 us
  waiting for transfers between devices: 129 us -> 0 us
  other arithmetic: 124 us -> 0.23 us
  between operations: 13.9 us -> 0.7 us
    dot_general x5 -> x0, matrix products: 195 us -> none  [the longest x1 54 us: local_layer(): jnp.einsum('bmn,bnd->bmd', mix_weights, all_slots, preferred_element_type...]
    pallas_call x0 -> x3, Pallas kernels: none -> 189 us  [the longest x1 94.8 us: experts(): pl.pallas_call(functools.partial(expert_kernel, n_group, n_chunk), out_sh...]
    psum x1 -> x0, blocking collectives: 148 us -> none  [local_layer(): lax.psum(out_part, 'model').astype(jnp.bfloat16)]
    reduce_scatter x1 -> x0, waiting for transfers between devices: 89.6 us -> none  [local_layer(): lax.psum_scatter(part_sum.astype(jnp.bfloat16), 'seq', scatter_dimension=...]
    sub x1 -> x0, other arithmetic: 69 us -> none  [local_layer(): mix_weights = jax.nn.softmax(logits, axis=-1).astype(jnp.bfloat16)]
    reduce_sum x2 -> x1, other arithmetic: 30.9 us -> 0.12 us  [unit_vectors(): jnp.sum(v32 * v32, axis=axis, keepdims=True) + NORM_EPS]
    pmax x1 -> x0, waiting for transfers between devices: 28.9 us -> none  [local_layer(): col_max = lax.pmax(jnp.max(masked, axis=1, keepdims=True), 'seq')]
    reduce_sum x1 -> x0, other arithmetic: 21.1 us -> none  [local_layer(): jnp.sum(weights, axis=1)]
  transfers between devices with their start and end apart: 4 -> 0, of which waited for: 3 -> 0; matrix products, arithmetic and copies ran while one was open for 19% -> 0% of each run, Pallas kernels for 0% -> 0%
where the time goes in v1:
time: 193 us; the launch traced here: 192 us
  Pallas kernels  189 us (98%)
  local copies, waits for them, and re-layouts  2.59 us (1%)
    pallas_call x1, Pallas kernels, experts(): pl.pallas_call(functools.partial(expert_kernel, n_group, n_chunk), out_sh...  94.8 us
    pallas_call x1, Pallas kernels, dispatch(): pl.pallas_call(functools.partial(dispatch_kernel, half), out_shape=pltpu....  66.6 us
    pallas_call x1, Pallas kernels, combine(): pl.pallas_call(functools.partial(combine_kernel, step), grid=(n_batch //...  27.2 us

profile of v1, /device:TPU:0, one launch (start us, length us, event | category | flops | bytes accessed | tf_op | source)
XLA Modules:
  0.0 192.2 jit_solution(2022777778338371543)
XLA Ops:
  0.7 1.1 copy.9
  1.7 0.1 fusion
  1.9 0.1 fusion.1
  2.0 0.8 copy.11.v_ref
  2.8 0.0 copy-start
  2.8 0.7 copy-done
  3.5 66.6 %dispatch.1.xs_ref = bf16[4096,384]{1,0:T(8,128)(2,1)S(1)} custom-call(bf16[64,1024,384]{2,1,0:T(8,128)(2,1)} %x_hbm.3, bf16[256,384]{1,0:T(8,128)(2,1)S(1)} %bitcast.8, s32[64]{0:T(128)S(1)} %copy-done, f32[1]{0:T(128)} %bitcast.3.kg_ref), custom_call_target="tpu_custom_call" | custom-call | tf_op jit(solution)/shard_map/dispatch/pallas_call | solution.py:184
  70.2 94.8 %experts.1 = (bf16[64,1024,256]{2,1,0:T(8,128)(2,1)S(1)}, bf16[64,256,384]{2,1,0:T(8,128)(2,1)}) custom-call(bf16[64,1024,384]{2,1,0:T(8,128)(2,1)} %x_hbm.3, bf16[384,256]{1,0:T(8,128)(2,1)} %copy.11.v_ref, s32[64]{0:T(128)} %len_ref.3, f32[1]{0:T(128)} %bitcast.3.kg_ref, bf16[4096,384]{1,0:T(8,128)(2,1)S(1)} %dispatch.1.xs_ref, ...), custom_call_target="tpu_custom_call" | custom-call | tf_op jit(solution)/shard_map/experts/pallas_call | solution.py:372
  164.9 27.2 %combine.1 = bf16[64,1024,384]{2,1,0:T(8,128)(2,1)} custom-call(bf16[64,1024,256]{2,1,0:T(8,128)(2,1)S(1)} %get-tuple-element.7.c_ref, bf16[64,256,384]{2,1,0:T(8,128)(2,1)} %get-tuple-element.8.ys_ref), custom_call_target="tpu_custom_call" | custom-call | tf_op jit(solution)/shard_map/combine/pallas_call | solution.py:403
  (2 shorter events, 0.0 us)
Async XLA Ops:
  2.8 0.7 copy-start

commit v2 on v1

v2 whole, which is shorter than its diff:
```python
import functools
import math
import jax
import jax.numpy as jnp
from jax import lax
from jax.experimental import pallas as pl
from jax.experimental.pallas import tpu as pltpu
from jax.sharding import PartitionSpec as P

NORM_EPS = 1e-6
LOG2E = math.log2(math.e)
MASKED = -1e30
MESH = pl.DeviceIdType.MESH
F32, BF16 = jnp.float32, jnp.bfloat16
NT = (((1,), (1,)), ((), ()))


def unit_columns(values):
    v32 = values.astype(F32)
    return v32 * lax.rsqrt(jnp.sum(v32 * v32, axis=0, keepdims=True) + NORM_EPS)


def place():
    y, s = lax.axis_index("model"), lax.axis_index("seq")
    x, core = s // 2, lax.rem(s, 2)
    partner = (0, y, x * 2 + 1 - core)
    across_x = (0, y, (1 - x) * 2 + core)
    across_y = (0, 1 - y, s)
    return y, x, core, s, partner, across_x, across_y


def greet(devices):
    barrier = pltpu.get_barrier_semaphore()
    for device in devices:
        pl.semaphore_signal(barrier, inc=1, device_id=device, device_id_type=MESH)
    pl.semaphore_wait(barrier, len(devices))


def remote(src, dst, send, recv, device):
    return pltpu.make_async_remote_copy(src_ref=src, dst_ref=dst, send_sem=send, recv_sem=recv, device_id=device, device_id_type=MESH)


def merge_weights(a, b):
    top = jnp.maximum(a, b)
    ea, eb = jnp.exp2(a - top), jnp.exp2(b - top)
    total = ea + eb
    row = lax.broadcasted_iota(jnp.int32, (8, a.shape[1]), 0)
    weights = jnp.where(row == 0, ea, eb) * (1.0 / total)
    return jnp.transpose(weights), top + jnp.log2(total)


def scatter_rows(acc, first, stride, rows):
    for j in range(acc.shape[0]):
        acc[j, pl.ds(first, rows.shape[0], stride=stride), :] = rows[:, j * 128 : (j + 1) * 128]


def gather_rows(acc, rows):
    return jnp.concatenate([acc[j, rows, :] for j in range(acc.shape[0])], axis=1)


def dispatch_kernel(half, pitch, x_hbm, phi_ref, len_ref, g_ref, xs_ref, vt_ref, xbuf, part, mid, xpart, own, yown, lse, dlse, mlse, xlse, wcol, in_sem, d_s, d_r, dl_s, dl_r, x_s, x_r, xl_s, xl_r, y_s, y_r):
    size = part.shape[0] // d_s.shape[0]
    n_step = half // size
    tok, n_slots, dim = xbuf.shape[1], vt_ref.shape[0], xbuf.shape[2]
    core_slots, dev_slots = n_slots // 2, n_slots // 4
    y, x, core, s, partner, across_x, across_y = place()
    base = y * half
    ring = xbuf.shape[0]
    kg = g_ref[0] * LOG2E

    def load(i):
        slot = lax.rem(i, ring)
        return pltpu.make_async_copy(x_hbm.at[base + i], xbuf.at[slot], in_sem.at[slot])

    def core_copy(u):
        rows, some = pl.ds(pl.multiple_of((1 - core) * core_slots, core_slots), core_slots), pl.ds(u * size, size)
        return remote(part.at[some, rows], mid.at[some], d_s.at[u], d_r.at[u], partner)

    def core_lse(u):
        some = pl.ds(u * size, size)
        return remote(lse.at[1 - core, some], dlse.at[some], dl_s.at[u], dl_r.at[u], partner)

    def x_copy(u):
        rows, some = pl.ds(pl.multiple_of((1 - x) * dev_slots, dev_slots), dev_slots), pl.ds(u * size, size)
        return remote(mid.at[some, rows], xpart.at[some], x_s.at[u], x_r.at[u], across_x)

    def x_lse(u):
        some = pl.ds(u * size, size)
        return remote(mlse.at[some], xlse.at[some], xl_s.at[u], xl_r.at[u], across_x)

    def y_copy(u):
        some = pl.ds(u * size, size)
        return remote(own.at[some], yown.at[some], y_s.at[u], y_r.at[u], across_y)

    for i in range(ring):
        load(i).start()
    v_rows = jnp.transpose(unit_columns(phi_ref[...]))
    for j, block in enumerate((0, 2, 1, 3)):
        vt_ref[j * dev_slots : (j + 1) * dev_slots] = v_rows[block * dev_slots : (block + 1) * dev_slots].astype(BF16)
    greet((partner, across_x, across_y))

    def local_mean(i):
        xv = xbuf[lax.rem(i, ring)]
        xf = xv.astype(F32)
        square = jnp.sum(xf * xf, axis=1, keepdims=True)
        square_row = jnp.transpose(jnp.broadcast_to(square, (tok, 128)))[0:1]
        scale_row = lax.rsqrt(square_row + NORM_EPS) * kg
        logits = lax.dot_general(vt_ref[...], xv, NT, preferred_element_type=F32) * scale_row
        lane = lax.broadcasted_iota(jnp.int32, (1, tok), 1)
        masked = jnp.where(lane < len_ref[base + i] - s * tok, logits, MASKED)
        top = jnp.max(masked, axis=1, keepdims=True)
        weights = jnp.exp2(masked - top)
        total = jnp.sum(weights, axis=1, keepdims=True)
        mean = jnp.dot(weights.astype(BF16), xv, preferred_element_type=F32) * (1.0 / total)
        part[i] = mean.astype(BF16)
        first = lax.broadcasted_iota(jnp.int32, (n_slots, 128), 1) == 0
        rows = jnp.transpose(jnp.where(first, top, total))
        row = rows[0:1] + jnp.log2(rows[1:2])
        lse[0, i] = row[:, :core_slots]
        lse[1, i] = row[:, core_slots:]

    def step(u, carry):
        @pl.when(u < n_step)
        def _():
            for j in range(size):
                load(u * size + j).wait()
            for j in range(size):
                local_mean(u * size + j)
            core_copy(u).start()
            core_lse(u).start()

            @pl.when(u * size + ring < half)
            def _():
                for j in range(size):
                    load(u * size + j + ring).start()

        @pl.when((u >= 1) & (u < n_step + 1))
        def _():
            core_copy(u - 1).wait_recv()
            core_lse(u - 1).wait_recv()
            rows = pl.ds(pl.multiple_of(core * core_slots, core_slots), core_slots)
            for j in range(size):
                k = (u - 1) * size + j
                cols, row = merge_weights(lse[core, k], dlse[k])
                merged = cols[:, 0:1] * part[k, rows].astype(F32) + cols[:, 1:2] * mid[k].astype(F32)
                mid[k] = merged.astype(BF16)
                mlse[k] = row
            x_copy(u - 1).start()
            x_lse(u - 1).start()

        @pl.when((u >= 3) & (u < n_step + 3))
        def _():
            x_copy(u - 3).wait_recv()
            x_lse(u - 3).wait_recv()
            rows = pl.ds(pl.multiple_of(x * dev_slots, dev_slots), dev_slots)
            for j in range(size):
                k = (u - 3) * size + j
                cols, _ = merge_weights(mlse[k], xlse[k])
                wcol[j] = cols
                mine = wcol[j, rows, :]
                merged = mine[:, 0:1] * mid[k, rows].astype(F32) + mine[:, 1:2] * xpart[k].astype(F32)
                own[k] = merged.astype(BF16)
                scatter_rows(xs_ref, base + k, pitch, merged)
            y_copy(u - 3).start()

        @pl.when(u >= 5)
        def _():
            y_copy(u - 5).wait_recv()
            for j in range(size):
                k = (u - 5) * size + j
                scatter_rows(xs_ref, (1 - y) * half + k, pitch, yown[k].astype(F32))

        return carry

    lax.fori_loop(0, n_step + 5, step, 0)

    def drain(u, carry):
        core_copy(u).wait_send()
        core_lse(u).wait_send()
        x_copy(u).wait_send()
        x_lse(u).wait_send()
        y_copy(u).wait_send()
        return carry

    lax.fori_loop(0, n_step, drain, 0)


def dispatch(tokens, phi, lengths, g, pitch):
    n_batch, tok, dim = tokens.shape
    n_slots = phi.shape[1]
    half, ring, size = n_batch // 2, 4, 2
    dma = pltpu.SemaphoreType.DMA
    return pl.pallas_call(
        functools.partial(dispatch_kernel, half, pitch),
        out_shape=pltpu.VMEM((dim // 128, n_slots // 4 * pitch, 128), F32),
        in_specs=[pl.BlockSpec(memory_space=pl.ANY), pl.BlockSpec(memory_space=pltpu.VMEM), pl.BlockSpec(memory_space=pltpu.SMEM), pl.BlockSpec(memory_space=pltpu.SMEM)],
        out_specs=pl.BlockSpec(memory_space=pltpu.VMEM),
        scratch_shapes=[
            pltpu.VMEM((n_slots, dim), BF16),
            pltpu.VMEM((ring, tok, dim), BF16),
            pltpu.VMEM((half, n_slots, dim), BF16),
            pltpu.VMEM((half, n_slots // 2, dim), BF16),
            pltpu.VMEM((half, n_slots // 4, dim), BF16),
            pltpu.VMEM((half, n_slots // 4, dim), BF16),
            pltpu.VMEM((half, n_slots // 4, dim), BF16),
            pltpu.VMEM((2, half, 1, n_slots // 2), F32),
            pltpu.VMEM((half, 1, n_slots // 2), F32),
            pltpu.VMEM((half, 1, n_slots // 2), F32),
            pltpu.VMEM((half, 1, n_slots // 2), F32),
            pltpu.VMEM((size, n_slots // 2, 8), F32),
            dma((ring,)),
        ] + [dma((half // size,))] * 10,
        compiler_params=pltpu.CompilerParams(collective_id=0, has_side_effects=True, vmem_limit_bytes=20 << 20),
        name="dispatch",
    )(tokens, phi, lengths, g)


def expert_kernel(n_group, n_chunk, pitch, x_hbm, phi_ref, len_ref, g_ref, xs_ref, win_hbm, wout_hbm, c_ref, ys_hbm, v_ref, xbuf, wi, wo, acc, ysend, yrecv, x_sem, wi_sem, wo_sem, y_s, y_r, x_s, x_r, d_s, d_r, r_s, r_r, l_s):
    n_batch, tok, dim = x_hbm.shape
    n_expert = win_hbm.shape[0]
    group = n_expert // n_group
    sub = n_batch // n_chunk
    kg = g_ref[0] * LOG2E
    y, x, core, s, partner, across_x, across_y = place()
    x_ring, w_ring = xbuf.shape[0], wi.shape[0]
    n_pair = n_expert // 2
    n_q = n_group * n_chunk

    def load_x(b):
        slot = lax.rem(b, x_ring)
        return pltpu.make_async_copy(x_hbm.at[b], xbuf.at[slot], x_sem.at[slot])

    def load_w(p):
        slot = lax.rem(p, w_ring)
        return (
            pltpu.make_async_copy(win_hbm.at[pl.ds(2 * p, 2)], wi.at[slot], wi_sem.at[slot]),
            pltpu.make_async_copy(wout_hbm.at[pl.ds(2 * p, 2)], wo.at[slot], wo_sem.at[slot]),
        )

    def home(q, on_core, on_x):
        g, bq = q // n_chunk, lax.rem(q, n_chunk)
        slot0 = pl.multiple_of((on_x * 2 + on_core) * n_expert + g * group, group)
        return ys_hbm.at[pl.ds(bq * sub, sub), pl.ds(slot0, group)]

    def y_copy(q):
        return remote(ysend.at[q], yrecv.at[q], y_s.at[q], y_r.at[q], across_y)

    def x_copy(q):
        return remote(yrecv.at[q], home(q, core, x), x_s.at[q], x_r.at[q], across_x)

    def x_arrival(q):
        return remote(yrecv.at[q], home(q, core, 1 - x), x_s.at[q], x_r.at[q], across_x)

    def core_copy(q):
        return remote(yrecv.at[q], home(q, core, x), d_s.at[q], d_r.at[q], partner)

    def core_arrival(q):
        return remote(yrecv.at[q], home(q, 1 - core, x), d_s.at[q], d_r.at[q], partner)

    def relay(q):
        return remote(home(q, core, 1 - x), home(q, core, 1 - x), r_s.at[q], r_r.at[q], partner)

    def relay_arrival(q):
        return remote(home(q, 1 - core, 1 - x), home(q, 1 - core, 1 - x), r_s.at[q], r_r.at[q], partner)

    def local_copy(q):
        return pltpu.make_async_copy(yrecv.at[q], home(q, core, x), l_s.at[q])

    for p in range(w_ring):
        for copy in load_w(p):
            copy.start()
    for b in range(x_ring):
        load_x(b).start()
    v_ref[...] = unit_columns(phi_ref[...]).astype(BF16)
    greet((partner, across_x, across_y))

    def expert_pair(p, carry):
        for copy in load_w(p):
            copy.wait()
        slot = lax.rem(p, w_ring)
        for j in range(2):
            e = 2 * p + j
            rows = gather_rows(xs_ref, pl.ds(pl.multiple_of(e * pitch, 8), n_batch)).astype(BF16)
            hidden = jnp.dot(rows, wi[slot, j], preferred_element_type=F32)
            hidden = (0.5 * hidden * (1.0 + lax.erf(hidden * math.sqrt(0.5)))).astype(BF16)
            out = jnp.dot(hidden, wo[slot, j], preferred_element_type=F32)
            scatter_rows(acc, lax.rem(e, group), group, out)

        @pl.when(p + w_ring < n_pair)
        def _():
            for copy in load_w(p + w_ring):
                copy.start()

        return carry

    def mix_block(b, carry):
        load_x(b).wait()
        slot = lax.rem(b, x_ring)
        xv = xbuf[slot]
        xf = xv.astype(F32)
        scale = lax.rsqrt(jnp.sum(xf * xf, axis=1, keepdims=True) + NORM_EPS) * kg
        logits = jnp.dot(xv, v_ref[...], preferred_element_type=F32) * scale
        weights = jnp.exp2(logits - jnp.max(logits, axis=1, keepdims=True))
        valid = lax.broadcasted_iota(jnp.int32, (tok, 1), 0) < len_ref[b] - s * tok
        inverse = jnp.where(valid, 1.0 / jnp.sum(weights, axis=1, keepdims=True), 0.0)
        c_ref[b] = (weights * inverse).astype(BF16)

        @pl.when(b + x_ring < n_batch)
        def _():
            load_x(b + x_ring).start()

        return carry

    per = n_expert // n_q
    lag = n_chunk + 1
    early, late = 3, 5

    def mix_start(t):
        first = jnp.maximum(t - n_chunk, 0) * early
        return jnp.minimum(jnp.where(t < n_q, first, (n_q - n_chunk) * early + (t - n_q) * late), n_batch)

    def step(t, carry):
        @pl.when(t < n_q)
        def _():
            lax.fori_loop(t * (per // 2), (t + 1) * (per // 2), expert_pair, 0)

        @pl.when((t < n_q) & (lax.rem(t, n_chunk) == n_chunk - 1))
        def _():
            g = t // n_chunk

            def pack(bq, carry):
                rows = gather_rows(acc, pl.ds(pl.multiple_of(bq * sub * group, sub * group), sub * group))
                q = g * n_chunk + bq
                ysend[q] = rows.reshape(sub, group, dim).astype(BF16)
                y_copy(q).start()
                return carry

            lax.fori_loop(0, n_chunk, pack, 0)

        lax.fori_loop(mix_start(t), mix_start(t + 1), mix_block, 0)

        @pl.when((t >= lag) & (t < n_q + lag))
        def _():
            q = t - lag
            y_copy(q).wait_recv()

            def add(i, carry):
                some = pl.ds(i * 8, 8)
                yrecv[q, some] = (ysend[q, some].astype(F32) + yrecv[q, some].astype(F32)).astype(BF16)
                return carry

            lax.fori_loop(0, sub // 8, add, 0)
            x_copy(q).start()
            core_copy(q).start()
            local_copy(q).start()

        @pl.when(t >= lag + 2)
        def _():
            q = t - lag - 2
            x_arrival(q).wait_recv()
            relay(q).start()

        return carry

    lax.fori_loop(0, n_q + lag + 2, step, 0)

    def drain(q, carry):
        core_arrival(q).wait_recv()
        relay_arrival(q).wait_recv()
        y_copy(q).wait_send()
        x_copy(q).wait_send()
        core_copy(q).wait_send()
        relay(q).wait_send()
        local_copy(q).wait()
        return carry

    lax.fori_loop(0, n_q, drain, 0)


def experts(tokens, phi, lengths, g, xs, w_in, w_out, pitch):
    n_batch, tok, dim = tokens.shape
    n_slots = phi.shape[1]
    n_expert, _, hid = w_in.shape
    n_group, n_chunk = 8, 2
    group, sub = n_expert // n_group, n_batch // n_chunk
    n_q = n_group * n_chunk
    x_ring, w_ring = 3, 3
    dma = pltpu.SemaphoreType.DMA
    vmem, smem, anym = pl.BlockSpec(memory_space=pltpu.VMEM), pl.BlockSpec(memory_space=pltpu.SMEM), pl.BlockSpec(memory_space=pl.ANY)
    return pl.pallas_call(
        functools.partial(expert_kernel, n_group, n_chunk, pitch),
        out_shape=(pltpu.VMEM((n_batch, tok, n_slots), BF16), jax.ShapeDtypeStruct((n_batch, n_slots, dim), BF16)),
        in_specs=[anym, vmem, smem, smem, vmem, anym, anym],
        out_specs=(vmem, anym),
        scratch_shapes=[
            pltpu.VMEM((dim, n_slots), BF16),
            pltpu.VMEM((x_ring, tok, dim), BF16),
            pltpu.VMEM((w_ring, 2, dim, hid), BF16),
            pltpu.VMEM((w_ring, 2, hid, dim), BF16),
            pltpu.VMEM((dim // 128, group * n_batch, 128), F32),
            pltpu.VMEM((n_q, sub, group, dim), BF16),
            pltpu.VMEM((n_q, sub, group, dim), BF16),
            dma((x_ring,)),
            dma((w_ring,)),
            dma((w_ring,)),
        ] + [dma((n_q,))] * 9,
        compiler_params=pltpu.CompilerParams(collective_id=1, has_side_effects=True, vmem_limit_bytes=18 << 20),
        name="experts",
    )(tokens, phi, lengths, g, xs, w_in, w_out)


def combine_kernel(c_ref, ys_hbm, y_hbm, ys, out, ys_sem, y_sem):
    n_batch, ring = c_ref.shape[0], out.shape[0]
    depth, step = ys.shape[0], ys.shape[1]
    n_group = n_batch // step

    def load(i):
        slot = lax.rem(i, depth)
        return pltpu.make_async_copy(ys_hbm.at[pl.ds(i * step, step)], ys.at[slot], ys_sem.at[slot])

    def store(b):
        slot = lax.rem(b, ring)
        return pltpu.make_async_copy(out.at[slot], y_hbm.at[b], y_sem.at[slot])

    for i in range(depth):
        load(i).start()

    def group(i, carry):
        load(i).wait()

        @pl.when(i * step >= ring)
        def _():
            for j in range(step):
                store(i * step + j - ring).wait()

        for j in range(step):
            b = i * step + j
            out[lax.rem(b, ring)] = jnp.dot(c_ref[b], ys[lax.rem(i, depth), j], preferred_element_type=F32).astype(BF16)
        for j in range(step):
            store(i * step + j).start()

        @pl.when(i + depth < n_group)
        def _():
            load(i + depth).start()

        return carry

    lax.fori_loop(0, n_group, group, 0)

    def drain(b, carry):
        store(b).wait()
        return carry

    lax.fori_loop(n_batch - ring, n_batch, drain, 0)


def combine(c, ys):
    n_batch, tok, n_slots = c.shape
    dim = ys.shape[2]
    step, depth, ring = 4, 4, 16
    return pl.pallas_call(
        combine_kernel,
        out_shape=jax.ShapeDtypeStruct((n_batch, tok, dim), BF16),
        in_specs=[pl.BlockSpec(memory_space=pltpu.VMEM), pl.BlockSpec(memory_space=pl.ANY)],
        out_specs=pl.BlockSpec(memory_space=pl.ANY),
        scratch_shapes=[
            pltpu.VMEM((depth, step, n_slots, dim), BF16),
            pltpu.VMEM((ring, tok, dim), BF16),
            pltpu.SemaphoreType.DMA((depth,)),
            pltpu.SemaphoreType.DMA((ring,)),
        ],
        compiler_params=pltpu.CompilerParams(vmem_limit_bytes=20 << 20),
        name="combine",
    )(c, ys)


def solution(mesh):
    def local_layer(tokens, lengths, slot_params, logit_scale, w_in, w_out):
        pitch = tokens.shape[0] + 8
        g = logit_scale.reshape(1)
        xs = dispatch(tokens, slot_params, lengths, g, pitch)
        c, ys = experts(tokens, slot_params, lengths, g, pltpu.with_memory_space_constraint(xs, pltpu.VMEM), w_in, w_out, pitch)
        return combine(pltpu.with_memory_space_constraint(c, pltpu.VMEM), ys)

    return jax.shard_map(local_layer, mesh=mesh, in_specs=(P("data", "seq", None), P("data"), P(), P(), P("seq", None, "model"), P("seq", "model", None)), out_specs=P("data", "seq", None), check_vma=False)
```

time: 193 us -> 162 us (0.84)
  Pallas kernels: 189 us -> 159 us
    pallas_call x3, Pallas kernels: 189 us -> 159 us  [the longest x1 84.3 us: experts(): pl.pallas_call(functools.partial(expert_kernel, n_group, n_chunk, pitch),...]
where the time goes in v2:
time: 162 us; the launch traced here: 161 us
  Pallas kernels  159 us (98%)
    pallas_call x1, Pallas kernels, experts(): pl.pallas_call(functools.partial(expert_kernel, n_group, n_chunk, pitch),...  84.3 us
    pallas_call x1, Pallas kernels, dispatch(): pl.pallas_call(functools.partial(dispatch_kernel, half, pitch), out_shape...  51.5 us
    pallas_call x1, Pallas kernels, combine(): pl.pallas_call(combine_kernel, out_shape=jax.ShapeDtypeStruct((n_batch, t...  23.3 us

profile of v2, /device:TPU:0, one launch (start us, length us, event | category | flops | bytes accessed | tf_op | source)
XLA Modules:
  0.0 161.4 jit_solution(3396164286747876311)
XLA Ops:
  0.7 0.0 copy-start
  0.7 0.9 copy-done
  1.6 0.0 copy-start.1
  1.6 0.7 copy-done.1
  2.2 51.5 %dispatch.1.xs_ref = f32[3,4608,128]{2,1,0:T(8,128)S(1)} custom-call(bf16[64,1024,384]{2,1,0:T(8,128)(2,1)} %x_hbm.3, bf16[384,256]{1,0:T(8,128)(2,1)S(1)} %copy-done, s32[64]{0:T(128)S(1)} %copy-done.1, f32[1]{0:T(128)} %bitcast.1.g_ref), custom_call_target="tpu_custom_call" | custom-call | tf_op jit(solution)/shard_map/dispatch/pallas_call | solution.py:193
  53.7 84.3 %experts.1 = (bf16[64,1024,256]{2,1,0:T(8,128)(2,1)S(1)}, bf16[64,256,384]{2,1,0:T(8,128)(2,1)}) custom-call(bf16[64,1024,384]{2,1,0:T(8,128)(2,1)} %x_hbm.3, bf16[384,256]{1,0:T(8,128)(2,1)} %phi_ref.3, s32[64]{0:T(128)} %len_ref.3, f32[1]{0:T(128)} %bitcast.2.g_ref, f32[3,4608,128]{2,1,0:T(8,128)S(1)} %dispatch.1.xs_ref, bf16[64,384,768]{2,1,0:T(8,128)(2,1)} %win_hbm.1, ...), custom_call_target="tpu_custom_call" | custom-call | tf_op jit(solution)/shard_map/experts/pallas_call | solution.py:390
  138.1 23.3 %combine.1 = bf16[64,1024,384]{2,1,0:T(8,128)(2,1)} custom-call(bf16[64,1024,256]{2,1,0:T(8,128)(2,1)S(1)} %get-tuple-element.7.c_ref, bf16[64,256,384]{2,1,0:T(8,128)(2,1)} %get-tuple-element.8.ys_hbm), custom_call_target="tpu_custom_call" | custom-call | tf_op jit(solution)/shard_map/combine/pallas_call | solution.py:461
Async XLA Ops:
  0.7 0.9 copy-start
  1.6 0.7 copy-start.1

commit v3 on v2

--- a/solution.py
+++ b/solution.py
@@ -40,6 +40,10 @@
     return pltpu.make_async_remote_copy(src_ref=src, dst_ref=dst, send_sem=send, recv_sem=recv, device_id=device, device_id_type=MESH)
 
 
+def small_copies(phi_hbm, phi_ref, len_hbm, len_ref, sem):
+    return pltpu.make_async_copy(phi_hbm, phi_ref, sem.at[0]), pltpu.make_async_copy(len_hbm, len_ref, sem.at[1])
+
+
 def merge_weights(a, b):
     top = jnp.maximum(a, b)
     ea, eb = jnp.exp2(a - top), jnp.exp2(b - top)
@@ -58,7 +62,7 @@
     return jnp.concatenate([acc[j, rows, :] for j in range(acc.shape[0])], axis=1)
 
 
-def dispatch_kernel(half, pitch, x_hbm, phi_ref, len_ref, g_ref, xs_ref, vt_ref, xbuf, part, mid, xpart, own, yown, lse, dlse, mlse, xlse, wcol, in_sem, d_s, d_r, dl_s, dl_r, x_s, x_r, xl_s, xl_r, y_s, y_r):
+def dispatch_kernel(half, pitch, x_hbm, phi_hbm, len_hbm, g_ref, xs_ref, phi_ref, len_ref, vt_ref, xbuf, part, mid, xpart, own, yown, lse, dlse, mlse, xlse, wcol, small_sem, in_sem, d_s, d_r, dl_s, dl_r, x_s, x_r, xl_s, xl_r, y_s, y_r):
     size = part.shape[0] // d_s.shape[0]
     n_step = half // size
     tok, n_slots, dim = xbuf.shape[1], vt_ref.shape[0], xbuf.shape[2]
@@ -92,12 +96,19 @@
         some = pl.ds(u * size, size)
         return remote(own.at[some], yown.at[some], y_s.at[u], y_r.at[u], across_y)
 
-    for i in range(ring):
+    small = small_copies(phi_hbm, phi_ref, len_hbm, len_ref, small_sem)
+    for copy in small:
+        copy.start()
+    for i in range(size):
         load(i).start()
+    for copy in small:
+        copy.wait()
     v_rows = jnp.transpose(unit_columns(phi_ref[...]))
     for j, block in enumerate((0, 2, 1, 3)):
         vt_ref[j * dev_slots : (j + 1) * dev_slots] = v_rows[block * dev_slots : (block + 1) * dev_slots].astype(BF16)
     greet((partner, across_x, across_y))
+    for i in range(size, ring):
+        load(i).start()
 
     def local_mean(i):
         xv = xbuf[lax.rem(i, ring)]
@@ -134,10 +145,11 @@
                 for j in range(size):
                     load(u * size + j + ring).start()
 
-        @pl.when((u >= 1) & (u < n_step + 1))
-        def _():
+        def core_wait():
             core_copy(u - 1).wait_recv()
             core_lse(u - 1).wait_recv()
+
+        def core_merge():
             rows = pl.ds(pl.multiple_of(core * core_slots, core_slots), core_slots)
             for j in range(size):
                 k = (u - 1) * size + j
@@ -145,13 +157,16 @@
                 merged = cols[:, 0:1] * part[k, rows].astype(F32) + cols[:, 1:2] * mid[k].astype(F32)
                 mid[k] = merged.astype(BF16)
                 mlse[k] = row
+
+        def core_send():
             x_copy(u - 1).start()
             x_lse(u - 1).start()
 
-        @pl.when((u >= 3) & (u < n_step + 3))
-        def _():
+        def x_wait():
             x_copy(u - 3).wait_recv()
             x_lse(u - 3).wait_recv()
+
+        def x_merge():
             rows = pl.ds(pl.multiple_of(x * dev_slots, dev_slots), dev_slots)
             for j in range(size):
                 k = (u - 3) * size + j
@@ -161,14 +176,41 @@
                 merged = mine[:, 0:1] * mid[k, rows].astype(F32) + mine[:, 1:2] * xpart[k].astype(F32)
                 own[k] = merged.astype(BF16)
                 scatter_rows(xs_ref, base + k, pitch, merged)
-            y_copy(u - 3).start()
-
-        @pl.when(u >= 5)
-        def _():
-            y_copy(u - 5).wait_recv()
+
+        def y_place():
             for j in range(size):
                 k = (u - 5) * size + j
                 scatter_rows(xs_ref, (1 - y) * half + k, pitch, yown[k].astype(F32))
+
+        steady = (u >= 5) & (u <= n_step)
+
+        @pl.when(steady)
+        def _():
+            core_wait()
+            x_wait()
+            y_copy(u - 5).wait_recv()
+            core_merge()
+            x_merge()
+            y_place()
+            core_send()
+            y_copy(u - 3).start()
+
+        @pl.when((u >= 1) & (u < 5))
+        def _():
+            core_wait()
+            core_merge()
+            core_send()
+
+        @pl.when((u >= 3) & (u < n_step + 3) & jnp.logical_not(steady))
+        def _():
+            x_wait()
+            x_merge()
+            y_copy(u - 3).start()
+
+        @pl.when(u > n_step)
+        def _():
+            y_copy(u - 5).wait_recv()
+            y_place()
 
         return carry
 
@@ -193,9 +235,11 @@
     return pl.pallas_call(
         functools.partial(dispatch_kernel, half, pitch),
         out_shape=pltpu.VMEM((dim // 128, n_slots // 4 * pitch, 128), F32),
-        in_specs=[pl.BlockSpec(memory_space=pl.ANY), pl.BlockSpec(memory_space=pltpu.VMEM), pl.BlockSpec(memory_space=pltpu.SMEM), pl.BlockSpec(memory_space=pltpu.SMEM)],
+        in_specs=[pl.BlockSpec(memory_space=pl.ANY)] * 3 + [pl.BlockSpec(memory_space=pltpu.SMEM)],
         out_specs=pl.BlockSpec(memory_space=pltpu.VMEM),
         scratch_shapes=[
+            pltpu.VMEM((dim, n_slots), BF16),
+            pltpu.SMEM((n_batch,), jnp.int32),
             pltpu.VMEM((n_slots, dim), BF16),
             pltpu.VMEM((ring, tok, dim), BF16),
             pltpu.VMEM((half, n_slots, dim), BF16),
@@ -208,6 +252,7 @@
             pltpu.VMEM((half, 1, n_slots // 2), F32),
             pltpu.VMEM((half, 1, n_slots // 2), F32),
             pltpu.VMEM((size, n_slots // 2, 8), F32),
+            dma((2,)),
             dma((ring,)),
         ] + [dma((half // size,))] * 10,
         compiler_params=pltpu.CompilerParams(collective_id=0, has_side_effects=True, vmem_limit_bytes=20 << 20),
@@ -215,14 +260,14 @@
     )(tokens, phi, lengths, g)
 
 
-def expert_kernel(n_group, n_chunk, pitch, x_hbm, phi_ref, len_ref, g_ref, xs_ref, win_hbm, wout_hbm, c_ref, ys_hbm, v_ref, xbuf, wi, wo, acc, ysend, yrecv, x_sem, wi_sem, wo_sem, y_s, y_r, x_s, x_r, d_s, d_r, r_s, r_r, l_s):
+def expert_kernel(n_group, n_chunk, pitch, x_hbm, phi_hbm, len_hbm, g_ref, xs_ref, win_hbm, wout_hbm, c_ref, ys_hbm, phi_ref, len_ref, v_ref, xbuf, wi, wo, acc, ysend, yrecv, small_sem, x_sem, wi_sem, wo_sem, y_s, y_r, x_s, x_r, d_s, d_r, r_s, r_r, l_s, f_s, f_r):
     n_batch, tok, dim = x_hbm.shape
     n_expert = win_hbm.shape[0]
     group = n_expert // n_group
     sub = n_batch // n_chunk
     kg = g_ref[0] * LOG2E
     y, x, core, s, partner, across_x, across_y = place()
-    x_ring, w_ring = xbuf.shape[0], wi.shape[0]
+    x_ring, w_ring, y_ring = xbuf.shape[0], wi.shape[0], ysend.shape[0]
     n_pair = n_expert // 2
     n_q = n_group * n_chunk
 
@@ -243,7 +288,11 @@
         return ys_hbm.at[pl.ds(bq * sub, sub), pl.ds(slot0, group)]
 
     def y_copy(q):
-        return remote(ysend.at[q], yrecv.at[q], y_s.at[q], y_r.at[q], across_y)
+        return remote(ysend.at[lax.rem(q, y_ring)], yrecv.at[q], y_s.at[q], y_r.at[q], across_y)
+
+    def first_copy(p, bq):
+        some, k = pl.ds(p * (sub // 4), sub // 4), p * n_chunk + bq
+        return remote(ysend.at[bq, some], yrecv.at[bq, some], f_s.at[k], f_r.at[k], across_y)
 
     def x_copy(q):
         return remote(yrecv.at[q], home(q, core, x), x_s.at[q], x_r.at[q], across_x)
@@ -266,13 +315,16 @@
     def local_copy(q):
         return pltpu.make_async_copy(yrecv.at[q], home(q, core, x), l_s.at[q])
 
-    for p in range(w_ring):
+    small = small_copies(phi_hbm, phi_ref, len_hbm, len_ref, small_sem)
+    for copy in (*small, *load_w(0)):
+        copy.start()
+    for copy in small:
+        copy.wait()
+    v_ref[...] = unit_columns(phi_ref[...]).astype(BF16)
+    greet((partner, across_x, across_y))
+    for p in range(1, w_ring):
         for copy in load_w(p):
             copy.start()
-    for b in range(x_ring):
-        load_x(b).start()
-    v_ref[...] = unit_columns(phi_ref[...]).astype(BF16)
-    greet((partner, across_x, across_y))
 
     def expert_pair(p, carry):
         for copy in load_w(p):
@@ -284,7 +336,15 @@
             hidden = jnp.dot(rows, wi[slot, j], preferred_element_type=F32)
             hidden = (0.5 * hidden * (1.0 + lax.erf(hidden * math.sqrt(0.5)))).astype(BF16)
             out = jnp.dot(hidden, wo[slot, j], preferred_element_type=F32)
-            scatter_rows(acc, lax.rem(e, group), group, out)
+            g, first = e // group, pl.multiple_of(lax.rem(e, group) * (sub // 8), sub // 8)
+            for bq in range(n_chunk):
+                piece = out[bq * sub : (bq + 1) * sub].astype(BF16)
+                ysend[lax.rem(g * n_chunk + bq, y_ring), pl.ds(first, sub // 8)] = piece.reshape(sub // 8, 8, dim)
+
+        @pl.when(p < group // 2)
+        def _():
+            for bq in range(n_chunk):
+                first_copy(p, bq).start()
 
         @pl.when(p + w_ring < n_pair)
         def _():
@@ -293,10 +353,8 @@
 
         return carry
 
-    def mix_block(b, carry):
-        load_x(b).wait()
-        slot = lax.rem(b, x_ring)
-        xv = xbuf[slot]
+    def mix_one(b):
+        xv = xbuf[lax.rem(b, x_ring)]
         xf = xv.astype(F32)
         scale = lax.rsqrt(jnp.sum(xf * xf, axis=1, keepdims=True) + NORM_EPS) * kg
         logits = jnp.dot(xv, v_ref[...], preferred_element_type=F32) * scale
@@ -305,69 +363,90 @@
         inverse = jnp.where(valid, 1.0 / jnp.sum(weights, axis=1, keepdims=True), 0.0)
         c_ref[b] = (weights * inverse).astype(BF16)
 
-        @pl.when(b + x_ring < n_batch)
-        def _():
-            load_x(b + x_ring).start()
+    def mix_pair(m, carry):
+        for j in range(2):
+            load_x(2 * m + j).wait()
+        for j in range(2):
+            mix_one(2 * m + j)
+
+        @pl.when(2 * m + x_ring < n_batch)
+        def _():
+            for j in range(2):
+                load_x(2 * m + j + x_ring).start()
 
         return carry
 
     per = n_expert // n_q
-    lag = n_chunk + 1
-    early, late = 3, 5
+    lag = 3
+    n_mix = n_batch // 2
+    early = 20
 
     def mix_start(t):
-        first = jnp.maximum(t - n_chunk, 0) * early
-        return jnp.minimum(jnp.where(t < n_q, first, (n_q - n_chunk) * early + (t - n_q) * late), n_batch)
+        first = jnp.maximum(t - n_chunk, 0) * early // (n_q - n_chunk)
+        rest = early + (t - n_q) * (n_mix - early) // (lag + 3)
+        return jnp.where(t < n_q, first, rest)
 
     def step(t, carry):
         @pl.when(t < n_q)
         def _():
             lax.fori_loop(t * (per // 2), (t + 1) * (per // 2), expert_pair, 0)
 
-        @pl.when((t < n_q) & (lax.rem(t, n_chunk) == n_chunk - 1))
-        def _():
-            g = t // n_chunk
-
-            def pack(bq, carry):
-                rows = gather_rows(acc, pl.ds(pl.multiple_of(bq * sub * group, sub * group), sub * group))
-                q = g * n_chunk + bq
-                ysend[q] = rows.reshape(sub, group, dim).astype(BF16)
-                y_copy(q).start()
-                return carry
-
-            lax.fori_loop(0, n_chunk, pack, 0)
-
-        lax.fori_loop(mix_start(t), mix_start(t + 1), mix_block, 0)
+        @pl.when((t >= n_chunk) & (t < n_q) & (lax.rem(t, n_chunk) == n_chunk - 1))
+        def _():
+            for bq in range(n_chunk):
+                y_copy(t - n_chunk + 1 + bq).start()
+
+        @pl.when(t == 0)
+        def _():
+            for b in range(x_ring):
+                load_x(b).start()
+
+        lax.fori_loop(mix_start(t), mix_start(t + 1), mix_pair, 0)
 
         @pl.when((t >= lag) & (t < n_q + lag))
         def _():
             q = t - lag
-            y_copy(q).wait_recv()
-
-            def add(i, carry):
-                some = pl.ds(i * 8, 8)
-                yrecv[q, some] = (ysend[q, some].astype(F32) + yrecv[q, some].astype(F32)).astype(BF16)
-                return carry
-
-            lax.fori_loop(0, sub // 8, add, 0)
+
+            @pl.when(q < n_chunk)
+            def _():
+                for p in range(group // 2):
+                    first_copy(p, q).wait_recv()
+
+            @pl.when(q >= n_chunk)
+            def _():
+                y_copy(q).wait_recv()
+
+            total = ysend[lax.rem(q, y_ring)].astype(F32) + yrecv[q].astype(F32)
+            total = total.reshape(group * sub, dim)
+            for e in range(group):
+                scatter_rows(acc, e, group, total[e * sub : (e + 1) * sub])
+            yrecv[q] = gather_rows(acc, pl.ds(0, group * sub)).reshape(sub, group, dim).astype(BF16)
             x_copy(q).start()
             core_copy(q).start()
             local_copy(q).start()
 
-        @pl.when(t >= lag + 2)
-        def _():
-            q = t - lag - 2
+            @pl.when(q < n_chunk)
+            def _():
+                for p in range(group // 2):
+                    first_copy(p, q).wait_send()
+
+            @pl.when(q >= n_chunk)
+            def _():
+                y_copy(q).wait_send()
+
+        @pl.when(t >= lag + 3)
+        def _():
+            q = t - lag - 3
             x_arrival(q).wait_recv()
             relay(q).start()
 
         return carry
 
-    lax.fori_loop(0, n_q + lag + 2, step, 0)
+    lax.fori_loop(0, n_q + lag + 3, step, 0)
 
     def drain(q, carry):
         core_arrival(q).wait_recv()
         relay_arrival(q).wait_recv()
-        y_copy(q).wait_send()
         x_copy(q).wait_send()
         core_copy(q).wait_send()
         relay(q).wait_send()
@@ -384,26 +463,29 @@
     n_group, n_chunk = 8, 2
     group, sub = n_expert // n_group, n_batch // n_chunk
     n_q = n_group * n_chunk
-    x_ring, w_ring = 3, 3
+    x_ring, w_ring = 4, 3
     dma = pltpu.SemaphoreType.DMA
     vmem, smem, anym = pl.BlockSpec(memory_space=pltpu.VMEM), pl.BlockSpec(memory_space=pltpu.SMEM), pl.BlockSpec(memory_space=pl.ANY)
     return pl.pallas_call(
         functools.partial(expert_kernel, n_group, n_chunk, pitch),
         out_shape=(pltpu.VMEM((n_batch, tok, n_slots), BF16), jax.ShapeDtypeStruct((n_batch, n_slots, dim), BF16)),
-        in_specs=[anym, vmem, smem, smem, vmem, anym, anym],
+        in_specs=[anym, anym, anym, smem, vmem, anym, anym],
         out_specs=(vmem, anym),
         scratch_shapes=[
+            pltpu.VMEM((dim, n_slots), BF16),
+            pltpu.SMEM((n_batch,), jnp.int32),
             pltpu.VMEM((dim, n_slots), BF16),
             pltpu.VMEM((x_ring, tok, dim), BF16),
             pltpu.VMEM((w_ring, 2, dim, hid), BF16),
             pltpu.VMEM((w_ring, 2, hid, dim), BF16),
-            pltpu.VMEM((dim // 128, group * n_batch, 128), F32),
+            pltpu.VMEM((dim // 128, group * sub, 128), F32),
+            pltpu.VMEM((n_q // 2, sub, group, dim), BF16),
             pltpu.VMEM((n_q, sub, group, dim), BF16),
-            pltpu.VMEM((n_q, sub, group, dim), BF16),
+            dma((2,)),
             dma((x_ring,)),
             dma((w_ring,)),
             dma((w_ring,)),
-        ] + [dma((n_q,))] * 9,
+        ] + [dma((n_q,))] * 9 + [dma((group // 2 * n_chunk,))] * 2,
         compiler_params=pltpu.CompilerParams(collective_id=1, has_side_effects=True, vmem_limit_bytes=18 << 20),
         name="experts",
     )(tokens, phi, lengths, g, xs, w_in, w_out)
@@ -478,8 +560,9 @@
     def local_layer(tokens, lengths, slot_params, logit_scale, w_in, w_out):
         pitch = tokens.shape[0] + 8
         g = logit_scale.reshape(1)
-        xs = dispatch(tokens, slot_params, lengths, g, pitch)
-        c, ys = experts(tokens, slot_params, lengths, g, pltpu.with_memory_space_constraint(xs, pltpu.VMEM), w_in, w_out, pitch)
+        phi, lens = (pltpu.with_memory_space_constraint(a, pltpu.HBM) for a in (slot_params, lengths))
+        xs = dispatch(tokens, phi, lens, g, pitch)
+        c, ys = experts(tokens, phi, lens, g, pltpu.with_memory_space_constraint(xs, pltpu.VMEM), w_in, w_out, pitch)
         return combine(pltpu.with_memory_space_constraint(c, pltpu.VMEM), ys)
 
     return jax.shard_map(local_layer, mesh=mesh, in_specs=(P("data", "seq", None), P("data"), P(), P(), P("seq", None, "model"), P("seq", "model", None)), out_specs=P("data", "seq", None), check_vma=False)

time: 162 us -> 158 us (0.975)
  no operation moved by 1% of the time
where the time goes in v3:
time: 158 us
  Pallas kernels  158 us (100%)
    pallas_call x1, Pallas kernels, experts(): pl.pallas_call(functools.partial(expert_kernel, n_group, n_chunk, pitch),...  83.7 us
    pallas_call x1, Pallas kernels, dispatch(): pl.pallas_call(functools.partial(dispatch_kernel, half, pitch), out_shape...  50.7 us
    pallas_call x1, Pallas kernels, combine(): pl.pallas_call(combine_kernel, out_shape=jax.ShapeDtypeStruct((n_batch, t...  23.3 us

profile of v3, /device:TPU:0, one launch (start us, length us, event | category | flops | bytes accessed | tf_op | source)
XLA Modules:
  0.0 158.3 jit_solution(17692003758978422952)
XLA Ops:
  0.7 50.7 %dispatch.1.xs_ref = f32[3,4608,128]{2,1,0:T(8,128)S(1)} custom-call(bf16[64,1024,384]{2,1,0:T(8,128)(2,1)} %x_hbm.3, bf16[384,256]{1,0:T(8,128)(2,1)} %phi_hbm.3, s32[64]{0:T(128)} %len_hbm.3, f32[1]{0:T(128)} %bitcast.1.g_ref), custom_call_target="tpu_custom_call" | custom-call | tf_op jit(solution)/shard_map/dispatch/pallas_call | solution.py:235
  51.4 83.7 %experts.1 = (bf16[64,1024,256]{2,1,0:T(8,128)(2,1)S(1)}, bf16[64,256,384]{2,1,0:T(8,128)(2,1)}) custom-call(bf16[64,1024,384]{2,1,0:T(8,128)(2,1)} %x_hbm.3, bf16[384,256]{1,0:T(8,128)(2,1)} %phi_hbm.3, s32[64]{0:T(128)} %len_hbm.3, f32[1]{0:T(128)} %bitcast.2.g_ref, f32[3,4608,128]{2,1,0:T(8,128)S(1)} %dispatch.1.xs_ref, bf16[64,384,768]{2,1,0:T(8,128)(2,1)} %win_hbm.1, ...), custom_call_target="tpu_custom_call" | custom-call | tf_op jit(solution)/shard_map/experts/pallas_call | solution.py:469
  135.0 23.3 %combine.1 = bf16[64,1024,384]{2,1,0:T(8,128)(2,1)} custom-call(bf16[64,1024,256]{2,1,0:T(8,128)(2,1)S(1)} %get-tuple-element.7.c_ref, bf16[64,256,384]{2,1,0:T(8,128)(2,1)} %get-tuple-element.8.ys_hbm), custom_call_target="tpu_custom_call" | custom-call | tf_op jit(solution)/shard_map/combine/pallas_call | solution.py:543

commit v4 on v3

--- a/solution.py
+++ b/solution.py
@@ -494,46 +494,40 @@
 def combine_kernel(c_ref, ys_hbm, y_hbm, ys, out, ys_sem, y_sem):
     n_batch, ring = c_ref.shape[0], out.shape[0]
     depth, step = ys.shape[0], ys.shape[1]
-    n_group = n_batch // step
-
-    def load(i):
-        slot = lax.rem(i, depth)
+    n_round = n_batch // ring
+
+    def load(i, slot):
         return pltpu.make_async_copy(ys_hbm.at[pl.ds(i * step, step)], ys.at[slot], ys_sem.at[slot])
 
-    def store(b):
-        slot = lax.rem(b, ring)
+    def store(b, slot):
         return pltpu.make_async_copy(out.at[slot], y_hbm.at[b], y_sem.at[slot])
 
     for i in range(depth):
-        load(i).start()
-
-    def group(i, carry):
-        load(i).wait()
-
-        @pl.when(i * step >= ring)
-        def _():
-            for j in range(step):
-                store(i * step + j - ring).wait()
-
-        for j in range(step):
-            b = i * step + j
-            out[lax.rem(b, ring)] = jnp.dot(c_ref[b], ys[lax.rem(i, depth), j], preferred_element_type=F32).astype(BF16)
-        for j in range(step):
-            store(i * step + j).start()
-
-        @pl.when(i + depth < n_group)
-        def _():
-            load(i + depth).start()
-
-        return carry
-
-    lax.fori_loop(0, n_group, group, 0)
-
-    def drain(b, carry):
-        store(b).wait()
-        return carry
-
-    lax.fori_loop(n_batch - ring, n_batch, drain, 0)
+        load(i, i).start()
+
+    def turn(r, carry):
+        for i in range(depth):
+            load(r * depth + i, i).wait()
+
+            @pl.when(r > 0)
+            def _():
+                for j in range(i * step, (i + 1) * step):
+                    store((r - 1) * ring + j, j).wait()
+
+            for j in range(i * step, (i + 1) * step):
+                out[j] = jnp.dot(c_ref[r * ring + j], ys[i, j - i * step], preferred_element_type=F32).astype(BF16)
+            for j in range(i * step, (i + 1) * step):
+                store(r * ring + j, j).start()
+
+            @pl.when(r < n_round - 1)
+            def _():
+                load((r + 1) * depth + i, i).start()
+
+        return carry
+
+    lax.fori_loop(0, n_round, turn, 0)
+    for j in range(ring):
+        store(n_batch - ring + j, j).wait()
 
 
 def combine(c, ys):

time: 158 us -> 158 us (level)
  no operation moved by 1% of the time
where the time goes in v4:
time: 158 us
  Pallas kernels  157 us (99%)
    pallas_call x1, Pallas kernels, experts(): pl.pallas_call(functools.partial(expert_kernel, n_group, n_chunk, pitch),...  83.7 us
    pallas_call x1, Pallas kernels, dispatch(): pl.pallas_call(functools.partial(dispatch_kernel, half, pitch), out_shape...  50.7 us
    pallas_call x1, Pallas kernels, combine(): pl.pallas_call(combine_kernel, out_shape=jax.ShapeDtypeStruct((n_batch, t...  23.1 us

profile of v4, /device:TPU:0, one launch (start us, length us, event | category | flops | bytes accessed | tf_op | source)
XLA Modules:
  0.0 158.2 jit_solution(13455549855676859154)
XLA Ops:
  0.7 50.7 %dispatch.1.xs_ref = f32[3,4608,128]{2,1,0:T(8,128)S(1)} custom-call(bf16[64,1024,384]{2,1,0:T(8,128)(2,1)} %x_hbm.3, bf16[384,256]{1,0:T(8,128)(2,1)} %phi_hbm.3, s32[64]{0:T(128)} %len_hbm.3, f32[1]{0:T(128)} %bitcast.1.g_ref), custom_call_target="tpu_custom_call" | custom-call | tf_op jit(solution)/shard_map/dispatch/pallas_call | solution.py:235
  51.4 83.7 %experts.1 = (bf16[64,1024,256]{2,1,0:T(8,128)(2,1)S(1)}, bf16[64,256,384]{2,1,0:T(8,128)(2,1)}) custom-call(bf16[64,1024,384]{2,1,0:T(8,128)(2,1)} %x_hbm.3, bf16[384,256]{1,0:T(8,128)(2,1)} %phi_hbm.3, s32[64]{0:T(128)} %len_hbm.3, f32[1]{0:T(128)} %bitcast.2.g_ref, f32[3,4608,128]{2,1,0:T(8,128)S(1)} %dispatch.1.xs_ref, bf16[64,384,768]{2,1,0:T(8,128)(2,1)} %win_hbm.1, ...), custom_call_target="tpu_custom_call" | custom-call | tf_op jit(solution)/shard_map/experts/pallas_call | solution.py:469
  135.0 23.1 %combine.1 = bf16[64,1024,384]{2,1,0:T(8,128)(2,1)} custom-call(bf16[64,1024,256]{2,1,0:T(8,128)(2,1)S(1)} %get-tuple-element.7.c_ref, bf16[64,256,384]{2,1,0:T(8,128)(2,1)} %get-tuple-element.8.ys_hbm), custom_call_target="tpu_custom_call" | custom-call | tf_op jit(solution)/shard_map/combine/pallas_call | solution.py:537

commit v5 on v4

--- a/solution.py
+++ b/solution.py
@@ -29,11 +29,14 @@
     return y, x, core, s, partner, across_x, across_y
 
 
+def announce(devices):
+    for device in devices:
+        pl.semaphore_signal(pltpu.get_barrier_semaphore(), inc=1, device_id=device, device_id_type=MESH)
+
+
 def greet(devices):
-    barrier = pltpu.get_barrier_semaphore()
-    for device in devices:
-        pl.semaphore_signal(barrier, inc=1, device_id=device, device_id_type=MESH)
-    pl.semaphore_wait(barrier, len(devices))
+    announce(devices)
+    pl.semaphore_wait(pltpu.get_barrier_semaphore(), len(devices))
 
 
 def remote(src, dst, send, recv, device):
@@ -321,7 +324,7 @@
     for copy in small:
         copy.wait()
     v_ref[...] = unit_columns(phi_ref[...]).astype(BF16)
-    greet((partner, across_x, across_y))
+    announce((partner, across_x, across_y))
     for p in range(1, w_ring):
         for copy in load_w(p):
             copy.start()
@@ -340,6 +343,10 @@
             for bq in range(n_chunk):
                 piece = out[bq * sub : (bq + 1) * sub].astype(BF16)
                 ysend[lax.rem(g * n_chunk + bq, y_ring), pl.ds(first, sub // 8)] = piece.reshape(sub // 8, 8, dim)
+
+        @pl.when(p == 0)
+        def _():
+            pl.semaphore_wait(pltpu.get_barrier_semaphore(), 3)
 
         @pl.when(p < group // 2)
         def _():

time: 158 us -> 157 us (level)
  no operation moved by 1% of the time
where the time goes in v5:
time: 157 us
  Pallas kernels  156 us (99%)
    pallas_call x1, Pallas kernels, experts(): pl.pallas_call(functools.partial(expert_kernel, n_group, n_chunk, pitch),...  82.6 us
    pallas_call x1, Pallas kernels, dispatch(): pl.pallas_call(functools.partial(dispatch_kernel, half, pitch), out_shape...  50.7 us
    pallas_call x1, Pallas kernels, combine(): pl.pallas_call(combine_kernel, out_shape=jax.ShapeDtypeStruct((n_batch, t...  23.1 us

profile of v5, /device:TPU:0, one launch (start us, length us, event | category | flops | bytes accessed | tf_op | source)
XLA Modules:
  0.0 157.1 jit_solution(1816270878396622219)
XLA Ops:
  0.7 50.7 %dispatch.1.xs_ref = f32[3,4608,128]{2,1,0:T(8,128)S(1)} custom-call(bf16[64,1024,384]{2,1,0:T(8,128)(2,1)} %x_hbm.3, bf16[384,256]{1,0:T(8,128)(2,1)} %phi_hbm.3, s32[64]{0:T(128)} %len_hbm.3, f32[1]{0:T(128)} %bitcast.1.g_ref), custom_call_target="tpu_custom_call" | custom-call | tf_op jit(solution)/shard_map/dispatch/pallas_call | solution.py:238
  51.4 82.6 %experts.1 = (bf16[64,1024,256]{2,1,0:T(8,128)(2,1)S(1)}, bf16[64,256,384]{2,1,0:T(8,128)(2,1)}) custom-call(bf16[64,1024,384]{2,1,0:T(8,128)(2,1)} %x_hbm.3, bf16[384,256]{1,0:T(8,128)(2,1)} %phi_hbm.3, s32[64]{0:T(128)} %len_hbm.3, f32[1]{0:T(128)} %bitcast.2.g_ref, f32[3,4608,128]{2,1,0:T(8,128)S(1)} %dispatch.1.xs_ref, bf16[64,384,768]{2,1,0:T(8,128)(2,1)} %win_hbm.1, ...), custom_call_target="tpu_custom_call" | custom-call | tf_op jit(solution)/shard_map/experts/pallas_call | solution.py:476
  134.0 23.1 %combine.1 = bf16[64,1024,384]{2,1,0:T(8,128)(2,1)} custom-call(bf16[64,1024,256]{2,1,0:T(8,128)(2,1)S(1)} %get-tuple-element.7.c_ref, bf16[64,256,384]{2,1,0:T(8,128)(2,1)} %get-tuple-element.8.ys_hbm), custom_call_target="tpu_custom_call" | custom-call | tf_op jit(solution)/shard_map/combine/pallas_call | solution.py:544
